TPU v7x, 32 devices: a whole 2x2x4 slice. The times are simulated.
32 devices in a mesh: tile: 8 (over y, x, core), layer: 4 (over z).
Axes of the slice: x: 2, y: 2, z: 4, core: 2. Of those that a mesh axis runs over, the one named last changes fastest.
Arguments:
- rand_vectors: bfloat16 [4, 16, 98304], P(None, None, ('tile', 'layer')), may hold values from -4 to 4
- onsite: bfloat16 [768, 128, 128], P(('tile', 'layer')), as said below
- down_hop: bfloat16 [768, 128, 128], P(('tile', 'layer')), may hold values from -0.1875 to 0.1875
- right_hop: bfloat16 [768, 128, 128], P(('tile', 'layer')), may hold values from -0.1875 to 0.1875
- pattern: int32 [768, 2], P(('tile', 'layer')), may hold values 0 or 1
- pairing: float32 [98304], P(('tile', 'layer')), may hold values from 0.1 to 1
- link_rows: int32 [256, 8], P(('tile', 'layer')), may hold values from 0 to 3071
- link_target: int32 [256, 8], P(('tile', 'layer')), may hold values from 0 to 3071
- link_weight: bfloat16 [256, 8], P(('tile', 'layer')), may hold values from -3 to 3
- link_count: int32 [256], P(('tile', 'layer')), may hold values from 0 to 8, as said below
Outputs:
- cheb_one: float32 [4, 16, 98304], P(None, None, ('tile', 'layer'))
- cheb_two: float32 [4, 16, 98304], P(None, None, ('tile', 'layer'))
- moments: float32 [3, 4, 98304], P(None, None, ('tile', 'layer'))
Inputs may be any that keep to these rules, and one draw needn't show every extreme that they name: `onsite`: every tile is symmetric. `link_rows`: a local site of the sending device. `link_target`: a local site of the receiving device. `link_count`: the number of used slots from one source tile row index to one receiving device; loads differ strongly between receiving tile row indices.
All inputs are finite; a program needn't handle non-finite values. No bound on the sum of `pattern` on one device may be relied on, other than what follows from the above.
Results may differ from a plain program's by a relative error of at most 0.0025.
Values may be sent and summed in bfloat16 or wider, within the bound.
A program may use at most 64 MiB of HBM per device.

v0:
```python
import jax
import jax.numpy as jnp
from jax import lax
from jax.sharding import PartitionSpec as P

TILE = 128
TR = 4
TC = 6


def partner_2(value, axis, bit):
    return lax.ppermute(value, axis, [(i, i ^ 1 << bit) for i in range(lax.axis_size(axis))])


def passed_along(value, axis, by):
    length = lax.axis_size(axis)
    pairs = [(i, i + by) for i in range(length) if 0 <= i + by < length]
    return lax.ppermute(value, axis, pairs)


def hop_forward(tiles, field_grid):
    return jnp.einsum("rkij,nrkj->nrki", tiles, field_grid, preferred_element_type=jnp.float32)


def hop_transposed(tiles, field_grid):
    return jnp.einsum("rkji,nrkj->nrki", tiles, field_grid, preferred_element_type=jnp.float32)


def shards(
    rand_vectors,
    onsite,
    down_hop,
    right_hop,
    pattern,
    pairing,
    link_rows,
    link_target,
    link_weight,
    link_count,
):
    components, vectors, sites_dev = rand_vectors.shape
    field_rows = components * vectors
    tile_count = lax.axis_size("tile")
    slot_count = link_rows.shape[1]
    self_tiles = onsite.reshape(TR, TC, TILE, TILE)
    down_mask = (down_hop * pattern[:, 0][:, None, None].astype(jnp.bfloat16)).reshape(
        TR, TC, TILE, TILE
    )
    right_mask = (right_hop * pattern[:, 1][:, None, None].astype(jnp.bfloat16)).reshape(
        TR, TC, TILE, TILE
    )
    is_left = lax.axis_index("layer") % 2 == 0
    slot_live = jnp.arange(slot_count, dtype=jnp.int32)[None, :] < link_count[:, None]
    slot_weight = jnp.where(slot_live, link_weight.astype(jnp.float32), 0.0).reshape(-1)
    send_rows = link_rows.reshape(-1)
    recv_sites = link_target.reshape(-1)
    weight_table = slot_weight.reshape(tile_count, slot_count).astype(jnp.bfloat16)
    weight_spread = lax.all_to_all(weight_table, "tile", split_axis=0, concat_axis=0, tiled=True)
    sender_weight = partner_2(weight_spread, "layer", 1).astype(jnp.float32).reshape(-1)

    def apply_hop(field_b):
        field_grid = field_b.reshape(field_rows, TR, TC, TILE)
        accumulated = hop_forward(self_tiles, field_grid)
        lower_row = passed_along(field_grid[:, :1], "tile", -1)
        accumulated = accumulated + hop_forward(
            down_mask, jnp.concatenate([field_grid[:, 1:], lower_row], axis=1)
        )
        upward = hop_transposed(down_mask, field_grid)
        upper_row = passed_along(upward[:, TR - 1 :], "tile", 1)
        accumulated = accumulated + jnp.concatenate([upper_row, upward[:, :-1]], axis=1)
        leftward = hop_transposed(right_mask, field_grid)
        payload = jnp.where(
            is_left, leftward[:, :, TC - 1], field_grid[:, :, 0].astype(jnp.float32)
        )
        partner = partner_2(payload, "layer", 0)
        right_edge = jnp.where(is_left, partner, 0.0).astype(jnp.bfloat16)
        accumulated = accumulated + hop_forward(
            right_mask, jnp.concatenate([field_grid[:, :, 1:], right_edge[:, :, None]], axis=2)
        )
        left_edge = jnp.where(is_left, 0.0, partner)
        accumulated = accumulated + jnp.concatenate(
            [left_edge[:, :, None], leftward[:, :, :-1]], axis=2
        )
        accumulated = accumulated.reshape(field_rows, sites_dev)
        flat_field = field_b.reshape(field_rows, sites_dev)
        outgoing = jnp.take(flat_field, send_rows, axis=1).reshape(
            field_rows, tile_count, slot_count
        )
        own_ends = jnp.take(flat_field, recv_sites, axis=1).reshape(
            field_rows, tile_count, slot_count
        )
        paired = jnp.concatenate([outgoing, own_ends], axis=2)
        paired_spread = lax.all_to_all(paired, "tile", split_axis=1, concat_axis=1, tiled=True)
        landed = partner_2(paired_spread, "layer", 1)
        arrived_terms = (
            landed[:, :, :slot_count].reshape(field_rows, -1).astype(jnp.float32)
            * slot_weight[None, :]
        )
        accumulated = accumulated.at[:, recv_sites].add(arrived_terms)
        returned_terms = (
            landed[:, :, slot_count:].reshape(field_rows, -1).astype(jnp.float32)
            * sender_weight[None, :]
        )
        accumulated = accumulated.at[:, send_rows].add(returned_terms)
        return accumulated.reshape(components, vectors, sites_dev)

    nambu_sign = jnp.array([1.0, 1.0, -1.0, -1.0], dtype=jnp.float32)[:, None, None]
    initial = rand_vectors.astype(jnp.float32)
    cheb_one = nambu_sign * apply_hop(rand_vectors) + pairing * jnp.roll(initial, 2, axis=0)
    one_rounded = cheb_one.astype(jnp.bfloat16)
    cheb_two = (
        2.0 * (nambu_sign * apply_hop(one_rounded) + pairing * jnp.roll(cheb_one, 2, axis=0))
        - initial
    )
    moments = jnp.stack(
        [
            jnp.mean(initial * initial, axis=1),
            jnp.mean(initial * cheb_one, axis=1),
            jnp.mean(initial * cheb_two, axis=1),
        ]
    )
    return (cheb_one, cheb_two, moments)


def solution(mesh):
    in_specs = (
        P(None, None, ("tile", "layer")),
        P(("tile", "layer"), None, None),
        P(("tile", "layer"), None, None),
        P(("tile", "layer"), None, None),
        P(("tile", "layer"), None),
        P(("tile", "layer")),
        P(("tile", "layer"), None),
        P(("tile", "layer"), None),
        P(("tile", "layer"), None),
        P(("tile", "layer")),
    )
    out_specs = (
        P(None, None, ("tile", "layer")),
        P(None, None, ("tile", "layer")),
        P(None, None, ("tile", "layer")),
    )
    return jax.shard_map(shards, mesh=mesh, in_specs=in_specs, out_specs=out_specs, check_vma=False)
```

profile of v0, /device:TPU:1, one launch (start us, length us, event | category | flops | bytes accessed | tf_op | source)
XLA Modules:
  0.0 108.2 jit_solution(1430978727805243666)
XLA Ops:
  3.7 2.1 %collective-permute-start.2 = (f32[64,4,128]{2,0,1:T(8,128)}, f32[64,4,128]{2,0,1:T(8,128)}, u32[]{:S(2)}, u32[]{:S(2)}) collective-permute-start(f32[64,4,128]{2,0,1:T(8,128)} %fusion.32), channel_id=1, source_target_pairs={{0,1},{1,0},{2,3},{3,2},{4,5},{5,4},{6,7},{7,6},{8,9},{9,8},{10,11... | collective-permute-start | bytes 393224 | tf_op jit(solution)/shard_map/ppermute | solution.py:12
  7.9 3.9 %collective-permute-start.1 = (f32[64,1,6,128]{3,0,2,1:T(8,128)}, f32[64,1,6,128]{3,0,2,1:T(8,128)}, u32[]{:S(2)}, u32[]{:S(2)}) collective-permute-start(f32[64,1,6,128]{3,0,2,1:T(8,128)} %slice.118), channel_id=1, source_target_pairs={{0,4},{4,8},{8,12},{12,16},{16,20},{20,24},{24,28},{1,5},{5,9},{9,... | collective-permute-start | bytes 589832 | tf_op jit(solution)/shard_map/ppermute | solution.py:18
  12.5 1.9 %collective-permute-start = (bf16[64,1,6,128]{3,0,2,1:T(8,128)(2,1)}, bf16[64,1,6,128]{3,0,2,1:T(8,128)(2,1)}, u32[]{:S(2)}, u32[]{:S(2)}) collective-permute-start(bf16[64,1,6,128]{3,0,2,1:T(8,128)(2,1)} %slice.117), channel_id=1, source_target_pairs={{4,0},{8,4},{12,8},{16,12},{20,16},{24,20},{28,24},{5,1},{9,5},{13... | collective-permute-start | bytes 294920 | tf_op jit(solution)/shard_map/ppermute | solution.py:18
  15.1 4.4 %all-to-all-start.1 = ((bf16[8,1,8]{2,1,0:T(2,128)(2,1)}), bf16[8,1,8]{2,1,0:T(2,128)(2,1)S(1)}, u32[]{:S(2)}, u32[]{:S(2)}) async-start(bf16[8,1,8]{2,1,0:T(2,128)(2,1)} %copy.111), calls=%async_computation.1 | async-start | bytes 8192 | tf_op jit(solution)/shard_map/all_to_all | solution.py:58
  23.4 1.8 %gather_fusion = bf16[64,64]{1,0:T(8,128)(2,1)S(1)} fusion(bf16[64,3072]{0,1:T(8,128)(2,1)} %copy.108, s32[1024]{0:T(1024)S(1)} %pad_clamp_fusion.1), kind=kCustom, calls=%fused_computation.clone | custom fusion | bytes 16640 | tf_op jit(solution)/shard_map/jit(_take)/gather | solution.py:86
  25.2 1.8 %gather_fusion.1 = bf16[64,64]{1,0:T(8,128)(2,1)S(1)} fusion(bf16[64,3072]{0,1:T(8,128)(2,1)} %copy.108, s32[1024]{0:T(1024)S(1)} %pad_clamp_fusion), kind=kCustom, calls=%fused_computation.1.clone | custom fusion | bytes 16640 | tf_op jit(solution)/shard_map/jit(_take)/gather | solution.py:89
  28.6 4.2 %all-to-all-start = ((bf16[8,2,512]{2,1,0:T(2,128)(2,1)}), bf16[8,2,512]{2,1,0:T(2,128)(2,1)S(1)}, u32[]{:S(2)}, u32[]{:S(2)}) async-start(bf16[8,2,512]{2,1,0:T(2,128)(2,1)} %reshape.301), calls=%async_computation | async-start | bytes 32768 | tf_op jit(solution)/shard_map/all_to_all | solution.py:93
  34.7 2.3 %collective-permute-start.4 = (bf16[8,8]{1,0:T(8,128)(2,1)S(1)}, bf16[8,8]{1,0:T(8,128)(2,1)S(1)}, u32[]{:S(2)}, u32[]{:S(2)}) collective-permute-start(bf16[8,8]{1,0:T(8,128)(2,1)S(1)} %bitcast.161), channel_id=1, source_target_pairs={{0,2},{1,3},{2,0},{3,1},{4,6},{5,7},{6,4},{7,5},{8,10},{9,11},{10,... | collective-permute-start | bytes 392 | tf_op jit(solution)/shard_map/ppermute | solution.py:12
  39.4 2.3 %collective-permute-start.3 = (bf16[64,8,16]{0,2,1:T(8,128)(2,1)}, bf16[64,8,16]{0,2,1:T(8,128)(2,1)}, u32[]{:S(2)}, u32[]{:S(2)}) collective-permute-start(bf16[64,8,16]{0,2,1:T(8,128)(2,1)} %bitcast.127), channel_id=1, source_target_pairs={{0,2},{1,3},{2,0},{3,1},{4,6},{5,7},{6,4},{7,5},{8,10},{9,11},{10,... | collective-permute-start | bytes 49160 | tf_op jit(solution)/shard_map/ppermute | solution.py:12
  43.3 2.5 %fusion.7 = f32[64,4,6,128]{3,0,2,1:T(8,128)} fusion(f32[64,4,6,128]{3,0,2,1:T(8,128)S(1)} %convolution_bitcast_fusion.5, f32[4,6,64,128]{3,2,1,0:T(8,128)S(1)} %copy-done.7, bf16[4,6,128,128]{3,2,1,0:T(8,128)(2,1)S(1)} %bitcast.150, f32[64,3,6,128]{3,0,2,1:T(8,128)S(1)} %slice-done.3, f32[64,1,6,128]{3,0,2,1:T(8,128)} %collective-permute-done.1, ...), kind=kOutput, calls=%fused_computation.24 | convolution fusion | flops 51707904 | bytes 5111808 | tf_op jit(solution)/shard_map/rkij,nrkj->nrki/dot_general | solution.py:22
  47.5 1.8 %scatter_custom_fusion = f32[64,3072]{0,1:T(8,128)S(1)} fusion(f32[64,3072]{0,1:T(8,128)S(1)} %bitcast.147, s32[64]{0:T(128)} %fusion.51, bf16[64,8,16]{0,2,1:T(8,128)(2,1)} %collective-permute-done.3, f32[64]{0:T(128)} %mul.125), kind=kCustom, calls=%fused_computation.84 | custom fusion | flops 12288 | bytes 803328 | tf_op jit(solution)/shard_map/scatter-add | solution.py:99
  52.5 2.6 %pad_maximum_fusion = (f32[4,16,3072]{2,1,0:T(8,128)}, f32[4,16,3072]{2,1,0:T(8,128)}) fusion(f32[2,16,3072]{2,1,0:T(8,128)} %get-tuple-element.13, f32[2,16,3072]{2,1,0:T(8,128)} %get-tuple-element.12, f32[3072]{0:T(1024)S(1)} %copy-done.14, f32[4,16,3072]{2,1,0:T(8,128)} %bitcast.160, f32[4]{0:T(128)} %constant.42.clone), kind=kLoop, calls=%fused_computation.25 | loop fusion | flops 786432 | bytes 3158032 | tf_op jit(solution)/shard_map/jit(_roll_static)/concatenate | solution.py:109
  55.1 2.8 %copy.127 = f32[64,3072]{0,1:T(8,128)} copy(f32[64,3072]{1,0:T(8,128)} %bitcast.158) | data formatting | bytes 1572864 | tf_op jit(solution)/shard_map/jit(_roll_static)/concatenate | solution.py:109
  57.9 2.8 %add_convert_fusion = bf16[64,3072]{0,1:T(8,128)(2,1)} fusion(f32[64,3072]{0,1:T(8,128)} %copy.127, f32[64,3072]{0,1:T(8,128)S(1)} %scatter_custom_fusion.1, f32[3072]{0:T(1024)S(1)} %copy-done.14, f32[64]{0:T(128)} %mul.136), kind=kLoop, calls=%fused_computation.8 | loop fusion | flops 786432 | bytes 1978624 | tf_op jit(solution)/shard_map/convert_element_type | solution.py:110
  60.7 2.4 %gather_fusion.2 = bf16[64,64]{1,0:T(8,128)(2,1)} fusion(bf16[64,3072]{0,1:T(8,128)(2,1)} %add_convert_fusion, s32[1024]{0:T(1024)S(1)} %pad_clamp_fusion.1), kind=kCustom, calls=%fused_computation.2.clone | custom fusion | bytes 16640 | tf_op jit(solution)/shard_map/jit(_take)/gather | solution.py:86
  63.1 2.6 %gather_fusion.3 = bf16[64,64]{1,0:T(8,128)(2,1)} fusion(bf16[64,3072]{0,1:T(8,128)(2,1)} %add_convert_fusion, s32[1024]{0:T(1024)} %copy-done.19), kind=kCustom, calls=%fused_computation.3.clone | custom fusion | bytes 16640 | tf_op jit(solution)/shard_map/jit(_take)/gather | solution.py:89
  65.6 2.5 %concatenate.47 = f32[64,4,6,128]{3,2,1,0:T(8,128)} reshape(f32[4,16,3072]{2,1,0:T(8,128)} %get-tuple-element.8) | data formatting | bytes 1572864 | tf_op jit(solution)/shard_map/jit(_roll_static)/concatenate | solution.py:109
  69.5 2.0 %fusion.14 = bf16[64,4,6,128]{3,0,1,2:T(8,128)(2,1)S(1)} fusion(f32[64,4,6,128]{3,2,1,0:T(8,128)} %concatenate.47, f32[64,4,6,128]{3,0,1,2:T(8,128)} %copy.114, f32[4,6,128]{2,0,1:T(4,128)} %copy.115, f32[64]{0:T(128)S(1)} %copy-done.22), kind=kLoop, calls=%fused_computation.34 | loop fusion | flops 786432 | bytes 1978624 | tf_op jit(solution)/shard_map/convert_element_type | solution.py:110
  75.0 5.6 %all-to-all-start.2 = ((bf16[8,2,512]{2,1,0:T(2,128)(2,1)}), bf16[8,2,512]{2,1,0:T(2,128)(2,1)S(1)}, u32[]{:S(2)}, u32[]{:S(2)}) async-start(bf16[8,2,512]{2,1,0:T(2,128)(2,1)} %reshape.303), calls=%async_computation.2 | async-start | bytes 32768 | tf_op jit(solution)/shard_map/all_to_all | solution.py:93
  82.5 2.1 %fusion.58 = (f32[2,16,3072]{2,1,0:T(8,128)}, f32[2,16,3072]{2,1,0:T(8,128)}) fusion(f32[4,16,3072]{2,1,0:T(8,128)} %get-tuple-element.9), kind=kLoop, calls=%fused_computation.117 | loop fusion | bytes 1572864 | tf_op jit(solution)/shard_map/jit(_roll_static)/slice | solution.py:112
  87.4 3.9 %collective-permute-start.6 = (f32[64,1,6,128]{3,0,1,2:T(8,128)}, f32[64,1,6,128]{3,0,1,2:T(8,128)}, u32[]{:S(2)}, u32[]{:S(2)}) collective-permute-start(f32[64,1,6,128]{3,0,1,2:T(8,128)} %slice.130), channel_id=1, source_target_pairs={{0,4},{4,8},{8,12},{12,16},{16,20},{20,24},{24,28},{1,5},{5,9},{9,... | collective-permute-start | bytes 589832 | tf_op jit(solution)/shard_map/ppermute | solution.py:18
  91.4 1.9 %collective-permute-start.5 = (bf16[64,1,6,128]{3,0,1,2:T(8,128)(2,1)}, bf16[64,1,6,128]{3,0,1,2:T(8,128)(2,1)}, u32[]{:S(2)}, u32[]{:S(2)}) collective-permute-start(bf16[64,1,6,128]{3,0,1,2:T(8,128)(2,1)} %slice.129), channel_id=1, source_target_pairs={{4,0},{8,4},{12,8},{16,12},{20,16},{24,20},{28,24},{5,1},{9,5},{13... | collective-permute-start | bytes 294920 | tf_op jit(solution)/shard_map/ppermute | solution.py:18
  95.8 1.8 %collective-permute-done.5 = bf16[64,1,6,128]{3,0,1,2:T(8,128)(2,1)} collective-permute-done((bf16[64,1,6,128]{3,0,1,2:T(8,128)(2,1)}, bf16[64,1,6,128]{3,0,1,2:T(8,128)(2,1)}, u32[]{:S(2)}, u32[]{:S(2)}) %collective-permute-start.5) | collective-permute-done | bytes 98336 | tf_op jit(solution)/shard_map/ppermute | solution.py:18
  104.9 2.6 %multiply_reduce_fusion.2 = (f32[4,3072]{1,0:T(4,128)S(1)}, f32[4,3072]{1,0:T(4,128)S(1)}, f32[4,3072]{1,0:T(4,128)S(1)}, f32[4,16,3072]{2,1,0:T(8,128)}) fusion(bf16[4,16,3072]{2,1,0:T(8,128)(2,1)S(1)} %copy-done.5, f32[4,16,3072]{2,1,0:T(8,128)S(1)} %copy-done.6, f32[2,16,3072]{2,1,0:T(8,128)} %get-tuple-element.11, f32[2,16,3072]{2,1,0:T(8,128)} %get-tuple-element.10, ...), kind=kLoop, calls=%fused_computation.37 | loop fusion | flops 2519040 | bytes 3698704 | tf_op jit(solution)/shard_map/reduce_sum | solution.py:117
  (160 shorter events, 42.0 us)
Async XLA Ops:
  0.6 20.1 %copy-start = (bf16[24,128,128]{2,1,0:T(8,128)(2,1)S(1)}, bf16[24,128,128]{2,1,0:T(8,128)(2,1)}, u32[]{:S(2)}) copy-start(bf16[24,128,128]{2,1,0:T(8,128)(2,1)} %param.14) | copy-start | bytes 2359300
  2.4 30.8 %copy-start.3 = (bf16[64,4,6,128]{3,0,2,1:T(8,128)(2,1)}, bf16[64,4,6,128]{3,0,2,1:T(8,128)(2,1)S(1)}, u32[]{:S(2)}) copy-start(bf16[64,4,6,128]{3,0,2,1:T(8,128)(2,1)S(1)} %copy.97) | copy-start | bytes 1179652
  2.6 40.0 %copy-start.1 = (bf16[24,128,128]{2,1,0:T(8,128)(2,1)}, bf16[24,128,128]{2,1,0:T(8,128)(2,1)S(1)}, u32[]{:S(2)}) copy-start(bf16[24,128,128]{2,1,0:T(8,128)(2,1)S(1)} %broadcast_multiply_fusion) | copy-start | bytes 2359300
  3.7 38.0 %collective-permute-start.2 = (f32[64,4,128]{2,0,1:T(8,128)}, f32[64,4,128]{2,0,1:T(8,128)}, u32[]{:S(2)}, u32[]{:S(2)}) collective-permute-start(f32[64,4,128]{2,0,1:T(8,128)} %fusion.32), channel_id=1, source_target_pairs={{0,1},{1,0},{2,3},{3,2},{4,5},{5,4},{6,7},{7,6},{8,9},{9,8},{10,11... | collective-permute-start | bytes 393224 | tf_op jit(solution)/shard_map/ppermute | solution.py:12
  5.9 8.5 %copy-start.29 = (bf16[8,8]{1,0:T(8,128)(2,1)S(1)}, bf16[8,8]{1,0:T(8,128)(2,1)}, u32[]{:S(2)}) copy-start(bf16[8,8]{1,0:T(8,128)(2,1)} %param.21) | copy-start | bytes 388
  5.9 8.5 %copy-start.30 = (s32[8]{0:T(128)S(1)}, s32[8]{0:T(128)}, u32[]{:S(2)}) copy-start(s32[8]{0:T(128)} %param.22) | copy-start | bytes 100
  5.9 13.5 %copy-start.17 = (s32[8,8]{1,0:T(8,128)S(1)}, s32[8,8]{1,0:T(8,128)}, u32[]{:S(2)}) copy-start(s32[8,8]{1,0:T(8,128)} %param.20) | copy-start | bytes 772
  5.9 13.6 %copy-start.18 = (s32[8,8]{1,0:T(8,128)S(1)}, s32[8,8]{1,0:T(8,128)}, u32[]{:S(2)}) copy-start(s32[8,8]{1,0:T(8,128)} %param.19) | copy-start | bytes 772
  6.0 13.8 %copy-start.5 = (bf16[4,16,3072]{2,1,0:T(8,128)(2,1)S(1)}, bf16[4,16,3072]{2,1,0:T(8,128)(2,1)}, u32[]{:S(2)}) copy-start(bf16[4,16,3072]{2,1,0:T(8,128)(2,1)} %param.13) | copy-start | bytes 1179652
  7.9 35.4 %collective-permute-start.1 = (f32[64,1,6,128]{3,0,2,1:T(8,128)}, f32[64,1,6,128]{3,0,2,1:T(8,128)}, u32[]{:S(2)}, u32[]{:S(2)}) collective-permute-start(f32[64,1,6,128]{3,0,2,1:T(8,128)} %slice.118), channel_id=1, source_target_pairs={{0,4},{4,8},{8,12},{12,16},{16,20},{20,24},{24,28},{1,5},{5,9},{9,... | collective-permute-start | bytes 589832 | tf_op jit(solution)/shard_map/ppermute | solution.py:18
  12.5 30.8 %collective-permute-start = (bf16[64,1,6,128]{3,0,2,1:T(8,128)(2,1)}, bf16[64,1,6,128]{3,0,2,1:T(8,128)(2,1)}, u32[]{:S(2)}, u32[]{:S(2)}) collective-permute-start(bf16[64,1,6,128]{3,0,2,1:T(8,128)(2,1)} %slice.117), channel_id=1, source_target_pairs={{4,0},{8,4},{12,8},{16,12},{20,16},{24,20},{28,24},{5,1},{9,5},{13... | collective-permute-start | bytes 294920 | tf_op jit(solution)/shard_map/ppermute | solution.py:18
  15.1 13.5 %all-to-all-start.1 = ((bf16[8,1,8]{2,1,0:T(2,128)(2,1)}), bf16[8,1,8]{2,1,0:T(2,128)(2,1)S(1)}, u32[]{:S(2)}, u32[]{:S(2)}) async-start(bf16[8,1,8]{2,1,0:T(2,128)(2,1)} %copy.111), calls=%async_computation.1 | async-start | bytes 8192 | tf_op jit(solution)/shard_map/all_to_all | solution.py:58
  23.4 9.9 %copy-start.19 = (s32[1024]{0:T(1024)}, s32[1024]{0:T(1024)S(1)}, u32[]{:S(2)}) copy-start(s32[1024]{0:T(1024)S(1)} %pad_clamp_fusion) | copy-start | bytes 12292
  28.6 10.1 %all-to-all-start = ((bf16[8,2,512]{2,1,0:T(2,128)(2,1)}), bf16[8,2,512]{2,1,0:T(2,128)(2,1)S(1)}, u32[]{:S(2)}, u32[]{:S(2)}) async-start(bf16[8,2,512]{2,1,0:T(2,128)(2,1)} %reshape.301), calls=%async_computation | async-start | bytes 32768 | tf_op jit(solution)/shard_map/all_to_all | solution.py:93
  33.3 10.0 %slice-start = ((bf16[64,4,6,128]{3,0,2,1:T(8,128)(2,1)}), bf16[64,3,6,128]{3,0,2,1:T(8,128)(2,1)S(1)}, s32[]{:S(2)}) async-start(bf16[64,4,6,128]{3,0,2,1:T(8,128)(2,1)} %copy-done.3), calls=%async_computation.3 | async-start | bytes 589824 | tf_op jit(solution)/shard_map/slice | solution.py:66
  34.7 3.3 %collective-permute-start.4 = (bf16[8,8]{1,0:T(8,128)(2,1)S(1)}, bf16[8,8]{1,0:T(8,128)(2,1)S(1)}, u32[]{:S(2)}, u32[]{:S(2)}) collective-permute-start(bf16[8,8]{1,0:T(8,128)(2,1)S(1)} %bitcast.161), channel_id=1, source_target_pairs={{0,2},{1,3},{2,0},{3,1},{4,6},{5,7},{6,4},{7,5},{8,10},{9,11},{10,... | collective-permute-start | bytes 392 | tf_op jit(solution)/shard_map/ppermute | solution.py:12
  39.4 8.1 %collective-permute-start.3 = (bf16[64,8,16]{0,2,1:T(8,128)(2,1)}, bf16[64,8,16]{0,2,1:T(8,128)(2,1)}, u32[]{:S(2)}, u32[]{:S(2)}) collective-permute-start(bf16[64,8,16]{0,2,1:T(8,128)(2,1)} %bitcast.127), channel_id=1, source_target_pairs={{0,2},{1,3},{2,0},{3,1},{4,6},{5,7},{6,4},{7,5},{8,10},{9,11},{10,... | collective-permute-start | bytes 49160 | tf_op jit(solution)/shard_map/ppermute | solution.py:12
  71.6 15.2 %copy-start.4 = (bf16[64,4,6,128]{3,0,1,2:T(8,128)(2,1)}, bf16[64,4,6,128]{3,0,1,2:T(8,128)(2,1)S(1)}, u32[]{:S(2)}) copy-start(bf16[64,4,6,128]{3,0,1,2:T(8,128)(2,1)S(1)} %fusion.14) | copy-start | bytes 1179652
  75.0 18.3 %all-to-all-start.2 = ((bf16[8,2,512]{2,1,0:T(2,128)(2,1)}), bf16[8,2,512]{2,1,0:T(2,128)(2,1)S(1)}, u32[]{:S(2)}, u32[]{:S(2)}) async-start(bf16[8,2,512]{2,1,0:T(2,128)(2,1)} %reshape.303), calls=%async_computation.2 | async-start | bytes 32768 | tf_op jit(solution)/shard_map/all_to_all | solution.py:93
  82.2 11.9 %collective-permute-start.7 = (f32[64,4,128]{2,0,1:T(8,128)}, f32[64,4,128]{2,0,1:T(8,128)}, u32[]{:S(2)}, u32[]{:S(2)}) collective-permute-start(f32[64,4,128]{2,0,1:T(8,128)} %fusion.31), channel_id=1, source_target_pairs={{0,1},{1,0},{2,3},{3,2},{4,5},{5,4},{6,7},{7,6},{8,9},{9,8},{10,11... | collective-permute-start | bytes 393224 | tf_op jit(solution)/shard_map/ppermute | solution.py:12
  87.4 10.2 %slice-start.1 = ((bf16[64,4,6,128]{3,0,1,2:T(8,128)(2,1)}), bf16[64,3,6,128]{3,0,1,2:T(8,128)(2,1)S(1)}, s32[]{:S(2)}) async-start(bf16[64,4,6,128]{3,0,1,2:T(8,128)(2,1)} %copy-done.4), calls=%async_computation.4 | async-start | bytes 589824 | tf_op jit(solution)/shard_map/slice | solution.py:66
  87.4 10.2 %collective-permute-start.6 = (f32[64,1,6,128]{3,0,1,2:T(8,128)}, f32[64,1,6,128]{3,0,1,2:T(8,128)}, u32[]{:S(2)}, u32[]{:S(2)}) collective-permute-start(f32[64,1,6,128]{3,0,1,2:T(8,128)} %slice.130), channel_id=1, source_target_pairs={{0,4},{4,8},{8,12},{12,16},{16,20},{20,24},{24,28},{1,5},{5,9},{9,... | collective-permute-start | bytes 589832 | tf_op jit(solution)/shard_map/ppermute | solution.py:18
  91.4 6.3 %collective-permute-start.5 = (bf16[64,1,6,128]{3,0,1,2:T(8,128)(2,1)}, bf16[64,1,6,128]{3,0,1,2:T(8,128)(2,1)}, u32[]{:S(2)}, u32[]{:S(2)}) collective-permute-start(bf16[64,1,6,128]{3,0,1,2:T(8,128)(2,1)} %slice.129), channel_id=1, source_target_pairs={{4,0},{8,4},{12,8},{16,12},{20,16},{24,20},{28,24},{5,1},{9,5},{13... | collective-permute-start | bytes 294920 | tf_op jit(solution)/shard_map/ppermute | solution.py:18
  94.0 5.8 %collective-permute-start.8 = (bf16[64,8,16]{0,2,1:T(8,128)(2,1)}, bf16[64,8,16]{0,2,1:T(8,128)(2,1)}, u32[]{:S(2)}, u32[]{:S(2)}) collective-permute-start(bf16[64,8,16]{0,2,1:T(8,128)(2,1)} %bitcast.129), channel_id=1, source_target_pairs={{0,2},{1,3},{2,0},{3,1},{4,6},{5,7},{6,4},{7,5},{8,10},{9,11},{10,... | collective-permute-start | bytes 49160 | tf_op jit(solution)/shard_map/ppermute | solution.py:12
  (26 other events, 74.2 us)
where the time goes:
time: 109 us; the launch traced here: 108 us
  local copies, waits for them, and re-layouts  36.2 us (33%)
  starting transfers between devices  32.9 us (30%)
  other arithmetic  23.9 us (22%)
  matrix products  11.6 us (11%)
  waiting for transfers between devices  2.28 us (2%)
  between operations  1.31 us (1%)
    ppermute x4, starting transfers between devices, passed_along(): return lax.ppermute(value, axis, pairs)  11.7 us
    all_to_all x2, starting transfers between devices, apply_hop(): lax.all_to_all(paired, 'tile', split_axis=1, concat_axis=1, tiled=True)  9.83 us
    dot_general x6, matrix products, hop_forward(): jnp.einsum('rkij,nrkj->nrki', tiles, field_grid, preferred_element_type=j...  8.48 us
    ppermute x5, starting transfers between devices, partner_2(): lax.ppermute(value, axis, [(i, i ^ 1 << bit) for i in range(lax.axis_size...  7.04 us
    concatenate x2, local copies, waits for them, and re-layouts, shards(): jnp.roll(initial, 2, axis=0)  5.31 us
    convert_element_type x2, other arithmetic, shards(): one_rounded = cheb_one.astype(jnp.bfloat16)  4.81 us
    gather x2, local copies, waits for them, and re-layouts, apply_hop(): jnp.take(flat_field, recv_sites, axis=1)  4.39 us
    all_to_all x1, starting transfers between devices, shards(): lax.all_to_all(weight_table, 'tile', split_axis=0, concat_axis=0, tiled=T...  4.36 us
  transfers between devices with their start and end apart: 12, of which 2 were waited for; matrix products, arithmetic and copies ran while one was open for 30% of the time, Pallas kernels for 0%

commit v1 on v0

v1 whole, which is shorter than its diff:
```python
import functools

import jax
import jax.numpy as jnp
from jax import lax
from jax.experimental import pallas as pl
from jax.experimental.pallas import tpu as pltpu
from jax.sharding import PartitionSpec as P

TR = 4
TC = 6
MESH = pl.DeviceIdType.MESH
F32 = jnp.float32
BF16 = jnp.bfloat16


def dot_nn(a, b):
    return lax.dot_general(a, b, (((1,), (0,)), ((), ())), preferred_element_type=F32)


def dot_nt(a, b):
    return lax.dot_general(a, b, (((1,), (1,)), ((), ())), preferred_element_type=F32)


def each(count, body):
    if count <= 16:
        for i in range(count):
            body(i)
    else:

        def step(i, carry):
            body(i)
            return carry

        lax.fori_loop(0, count, step, 0)


def kernel(
    n,
    nl,
    x_hbm,
    on_hbm,
    down_hbm,
    right_hbm,
    pat_ref,
    pair_ref,
    rows_ref,
    target_ref,
    weight_ref,
    count_ref,
    one_ref,
    two_ref,
    mom_ref,
    x_ref,
    on_ref,
    down_ref,
    right_ref,
    acc_ref,
    oneb_ref,
    hot_ref,
    idx_ref,
    wsend_ref,
    wloc_ref,
    gath_ref,
    wide_ref,
    sbuf,
    lbuf,
    pbuf,
    low_in,
    up_in,
    cbuf,
    col_in,
    load_sem,
    link_send,
    link_recv,
    edge_send,
    edge_recv,
):
    t = lax.axis_index("tile")
    l = lax.axis_index("layer")
    far = lax.rem(l + nl // 2, nl)
    is_left = lax.rem(l, 2) == 0
    partner = l + 1 - 2 * lax.rem(l, 2)
    fr, sites = x_ref.shape
    tile = on_ref.shape[1]
    tiles = sites // tile
    cap = rows_ref.shape[1]
    slots = n * 2 * cap
    wide = TC * tile

    loads = [
        pltpu.make_async_copy(x_hbm, x_ref, load_sem.at[0]),
        pltpu.make_async_copy(down_hbm, down_ref, load_sem.at[1]),
        pltpu.make_async_copy(right_hbm, right_ref, load_sem.at[2]),
        pltpu.make_async_copy(on_hbm, on_ref, load_sem.at[3]),
    ]
    for load in loads:
        load.start()

    has_up = t > 0
    has_low = t < n - 1
    barrier = pltpu.get_barrier_semaphore()
    each(
        n,
        lambda s: pl.semaphore_signal(barrier, inc=1, device_id=(s, far), device_id_type=MESH),
    )
    pl.semaphore_signal(barrier, inc=1, device_id=(t, partner), device_id_type=MESH)

    @pl.when(has_up)
    def _():
        pl.semaphore_signal(barrier, inc=1, device_id=(t - 1, l), device_id_type=MESH)

    @pl.when(has_low)
    def _():
        pl.semaphore_signal(barrier, inc=1, device_id=(t + 1, l), device_id_type=MESH)

    @pl.when(jnp.logical_not(has_up))
    def _():
        up_in[...] = jnp.zeros_like(up_in)

    @pl.when(jnp.logical_not(has_low))
    def _():
        low_in[...] = jnp.zeros_like(low_in)

    sub = lax.broadcasted_iota(jnp.int32, (cap, cap), 0)
    lane = lax.broadcasted_iota(jnp.int32, (cap, cap), 1)
    eye = sub == lane
    half = lax.broadcasted_iota(jnp.int32, (cap, 2 * fr), 1) >= fr

    wide_ref[...] = weight_ref[...].astype(F32)

    def columns(s):
        def column(row):
            spread = jnp.broadcast_to(row.astype(F32), (cap, cap))
            return jnp.sum(jnp.where(eye, spread, 0.0), axis=1, keepdims=True)

        base = s * (2 * cap)
        out_col = column(rows_ref[pl.ds(s, 1), :])
        own_col = column(target_ref[pl.ds(s, 1), :])
        idx_ref[pl.ds(base, cap), :] = jnp.broadcast_to(out_col, (cap, tile)).astype(jnp.int32)
        idx_ref[pl.ds(base + cap, cap), :] = jnp.broadcast_to(own_col, (cap, tile)).astype(
            jnp.int32
        )
        live = lax.broadcasted_iota(jnp.int32, (1, cap), 1) < count_ref[s]
        w_col = column(jnp.where(live, wide_ref[pl.ds(s, 1), :], 0.0))
        w_wide = jnp.where(half, jnp.broadcast_to(w_col, (cap, 2 * fr)), 0.0)
        zero = jnp.zeros_like(w_wide)
        wsend_ref[pl.ds(base, cap), :] = w_wide
        wsend_ref[pl.ds(base + cap, cap), :] = zero
        wloc_ref[pl.ds(base, cap), :] = zero
        wloc_ref[pl.ds(base + cap, cap), :] = w_wide

    each(n, columns)
    gath_ref[...] = jnp.zeros_like(gath_ref)

    lanes = lax.broadcasted_iota(jnp.int32, (slots, tile), 1)
    for p in range(tiles):
        hot = jnp.where(idx_ref[...] == lanes + p * tile, 1.0, 0.0)
        hot_ref[:, p * tile : (p + 1) * tile] = hot.astype(BF16)

    def block(ref, p):
        return ref[:, p * tile : (p + 1) * tile]

    def link_copy(rd, s, mine):
        return pltpu.make_async_remote_copy(
            src_ref=sbuf.at[rd, s],
            dst_ref=lbuf.at[rd, mine],
            send_sem=link_send.at[rd, s],
            recv_sem=link_recv.at[rd, mine],
            device_id=(s, far),
            device_id_type=MESH,
        )

    def field_copy(rd, src):
        return pltpu.make_async_remote_copy(
            src_ref=src.at[:, 0:wide],
            dst_ref=low_in.at[rd],
            send_sem=edge_send.at[rd, 0],
            recv_sem=edge_recv.at[rd, 0],
            device_id=(t - 1, l),
            device_id_type=MESH,
        )

    def partial_copy(rd):
        return pltpu.make_async_remote_copy(
            src_ref=pbuf.at[rd],
            dst_ref=up_in.at[rd],
            send_sem=edge_send.at[rd, 1],
            recv_sem=edge_recv.at[rd, 1],
            device_id=(t + 1, l),
            device_id_type=MESH,
        )

    def column_copy(rd):
        return pltpu.make_async_remote_copy(
            src_ref=cbuf.at[rd],
            dst_ref=col_in.at[rd],
            send_sem=edge_send.at[rd, 2],
            recv_sem=edge_recv.at[rd, 2],
            device_id=(t, partner),
            device_id_type=MESH,
        )

    def gather(rd, src):
        gath_ref[:, 0:fr] = dot_nt(hot_ref[...], src[...])

        def fill(s):
            base = s * (2 * cap)
            both = jnp.concatenate(
                [gath_ref[pl.ds(base + cap, cap), :], gath_ref[pl.ds(base, cap), :]], axis=0
            )
            sbuf[rd, s] = (both + wsend_ref[pl.ds(base, 2 * cap), :]).astype(BF16)

        each(n, fill)

    def edges(rd, src):
        for k in range(TC):
            p = (TR - 1) * TC + k
            pbuf[rd, :, k * tile : (k + 1) * tile] = dot_nn(block(src, p), down_ref[p]).astype(
                BF16
            )
        for r in range(TR):
            p = r * TC + TC - 1
            passed = dot_nn(block(src, p), right_ref[p])
            own = block(src, r * TC).astype(F32)
            cbuf[rd, :, r * tile : (r + 1) * tile] = jnp.where(is_left, passed, own).astype(BF16)

    def send_links(rd):
        each(n, lambda s: link_copy(rd, s, t).start())

    def send_edges(rd, src):
        column_copy(rd).start()

        @pl.when(has_up)
        def _():
            field_copy(rd, src).start()

        @pl.when(has_low)
        def _():
            partial_copy(rd).start()

    def local(src):
        for r in range(TR):
            for k in range(TC):
                p = r * TC + k
                ins = [block(src, p)]
                mats = [on_ref[p]]
                if r > 0:
                    ins.append(block(src, p - TC))
                    mats.append(down_ref[p - TC])
                if k > 0:
                    ins.append(block(src, p - 1))
                    mats.append(right_ref[p - 1])
                total = dot_nn(jnp.concatenate(ins, axis=1), jnp.concatenate(mats, axis=0))
                ins, mats = [], []
                if r < TR - 1:
                    ins.append(block(src, p + TC))
                    mats.append(down_ref[p])
                if k < TC - 1:
                    ins.append(block(src, p + 1))
                    mats.append(right_ref[p])
                if ins:
                    total = total + dot_nt(
                        jnp.concatenate(ins, axis=1), jnp.concatenate(mats, axis=1)
                    )
                acc_ref[:, p * tile : (p + 1) * tile] = total

    def receive_edges(rd):
        @pl.when(has_low)
        def _():
            field_copy(rd, x_ref).wait_recv()

        @pl.when(has_up)
        def _():
            partial_copy(rd).wait_recv()

        column_copy(rd).wait_recv()

    def add_edges(rd):
        for k in range(TC):
            cols = slice(k * tile, (k + 1) * tile)
            acc_ref[:, cols] += up_in[rd, :, cols].astype(F32)
            p = (TR - 1) * TC + k
            acc_ref[:, p * tile : (p + 1) * tile] += dot_nt(low_in[rd, :, cols], down_ref[p])
        for r in range(TR):
            arrived = col_in[rd, :, r * tile : (r + 1) * tile].astype(F32)
            p = r * TC
            acc_ref[:, p * tile : (p + 1) * tile] += jnp.where(is_left, 0.0, arrived)
            p = r * TC + TC - 1
            field = jnp.where(is_left, arrived, 0.0).astype(BF16)
            acc_ref[:, p * tile : (p + 1) * tile] += dot_nt(field, right_ref[p])

    def link_terms(rd):
        each(n, lambda s: link_copy(rd, s, s).wait_recv())
        landed = lbuf[rd].reshape(slots, 2 * fr).astype(F32) + wloc_ref[...]
        turned = landed.T
        terms = turned[0:fr] * turned[fr : 2 * fr]
        high = terms.astype(BF16)
        low = (terms - high.astype(F32)).astype(BF16)
        return jnp.concatenate([high, low], axis=0)

    sign = jnp.where(lax.broadcasted_iota(jnp.int32, (fr, tile), 0) < fr // 2, 1.0, -1.0)

    def flipped(v):
        return jnp.concatenate([v[fr // 2 :], v[: fr // 2]], axis=0)

    def scattered(terms, p):
        both = dot_nn(terms, block(hot_ref, p))
        return both[0:fr] + both[fr : 2 * fr]

    loads[0].wait()
    gather(0, x_ref)
    loads[1].wait()
    loads[2].wait()
    for p in range(tiles):
        down_ref[p] = down_ref[p] * pat_ref[p, 0].astype(F32).astype(BF16)
        right_ref[p] = right_ref[p] * pat_ref[p, 1].astype(F32).astype(BF16)
    edges(0, x_ref)
    pl.semaphore_wait(barrier, n + 1 + has_up.astype(jnp.int32) + has_low.astype(jnp.int32))
    send_links(0)
    send_edges(0, x_ref)
    loads[3].wait()
    local(x_ref)
    receive_edges(0)
    add_edges(0)
    terms = link_terms(0)
    for p in range(tiles):
        cols = slice(p * tile, (p + 1) * tile)
        hop = acc_ref[:, cols] + scattered(terms, p)
        start = x_ref[:, cols].astype(F32)
        one = sign * hop + pair_ref[:, cols] * flipped(start)
        one_ref[:, cols] = one
        oneb_ref[:, cols] = one.astype(BF16)

    gather(1, oneb_ref)
    send_links(1)
    edges(1, oneb_ref)
    send_edges(1, oneb_ref)
    local(oneb_ref)
    receive_edges(1)
    add_edges(1)
    terms = link_terms(1)
    comps, vecs = mom_ref.shape[1], fr // mom_ref.shape[1]

    def mean(v):
        return jnp.sum(v.reshape(comps, vecs, tile), axis=1) * (1.0 / vecs)

    for p in range(tiles):
        cols = slice(p * tile, (p + 1) * tile)
        hop = acc_ref[:, cols] + scattered(terms, p)
        start = x_ref[:, cols].astype(F32)
        one = one_ref[:, cols]
        two = 2.0 * (sign * hop + pair_ref[:, cols] * flipped(one)) - start
        two_ref[:, cols] = two
        mom_ref[0, :, cols] = mean(start * start)
        mom_ref[1, :, cols] = mean(start * one)
        mom_ref[2, :, cols] = mean(start * two)

    for rd in range(2):
        each(n, lambda s: link_copy(rd, s, t).wait_send())
        column_copy(rd).wait_send()

        @pl.when(has_up)
        def _():
            field_copy(rd, x_ref).wait_send()

        @pl.when(has_low)
        def _():
            partial_copy(rd).wait_send()


def shards(
    n,
    nl,
    rand_vectors,
    onsite,
    down_hop,
    right_hop,
    pattern,
    pairing,
    link_rows,
    link_target,
    link_weight,
    link_count,
):
    comps, vecs, sites = rand_vectors.shape
    fr = comps * vecs
    tiles, tile, _ = onsite.shape
    cap = link_rows.shape[1]
    slots = 2 * n * cap
    wide, tall = TC * tile, TR * tile
    vmem = pl.BlockSpec(memory_space=pltpu.VMEM)
    smem = pl.BlockSpec(memory_space=pltpu.SMEM)
    hbm = pl.BlockSpec(memory_space=pl.ANY)
    one, two, moments = pl.pallas_call(
        functools.partial(kernel, n, nl),
        out_shape=(
            jax.ShapeDtypeStruct((fr, sites), F32),
            jax.ShapeDtypeStruct((fr, sites), F32),
            jax.ShapeDtypeStruct((3, comps, sites), F32),
        ),
        in_specs=[hbm, hbm, hbm, hbm, smem, vmem, vmem, vmem, vmem, smem],
        out_specs=(vmem, vmem, vmem),
        scratch_shapes=[
            pltpu.VMEM((fr, sites), BF16),
            pltpu.VMEM((tiles, tile, tile), BF16),
            pltpu.VMEM((tiles, tile, tile), BF16),
            pltpu.VMEM((tiles, tile, tile), BF16),
            pltpu.VMEM((fr, sites), F32),
            pltpu.VMEM((fr, sites), BF16),
            pltpu.VMEM((slots, sites), BF16),
            pltpu.VMEM((slots, tile), jnp.int32),
            pltpu.VMEM((slots, 2 * fr), F32),
            pltpu.VMEM((slots, 2 * fr), F32),
            pltpu.VMEM((slots, 2 * fr), F32),
            pltpu.VMEM((n, cap), F32),
            pltpu.VMEM((2, n, 2 * cap, 2 * fr), BF16),
            pltpu.VMEM((2, n, 2 * cap, 2 * fr), BF16),
            pltpu.VMEM((2, fr, wide), BF16),
            pltpu.VMEM((2, fr, wide), BF16),
            pltpu.VMEM((2, fr, wide), BF16),
            pltpu.VMEM((2, fr, tall), BF16),
            pltpu.VMEM((2, fr, tall), BF16),
            pltpu.SemaphoreType.DMA((4,)),
            pltpu.SemaphoreType.DMA((2, n)),
            pltpu.SemaphoreType.DMA((2, n)),
            pltpu.SemaphoreType.DMA((2, 3)),
            pltpu.SemaphoreType.DMA((2, 3)),
        ],
        compiler_params=pltpu.CompilerParams(
            collective_id=0, has_side_effects=True, vmem_limit_bytes=56 * 1024 * 1024
        ),
    )(
        rand_vectors.reshape(fr, sites),
        onsite,
        down_hop,
        right_hop,
        pattern,
        pairing.reshape(1, sites),
        link_rows,
        link_target,
        link_weight,
        link_count,
    )
    return (
        one.reshape(comps, vecs, sites),
        two.reshape(comps, vecs, sites),
        moments,
    )


def solution(mesh):
    spread = ("tile", "layer")
    in_specs = (
        P(None, None, spread),
        P(spread, None, None),
        P(spread, None, None),
        P(spread, None, None),
        P(spread, None),
        P(spread),
        P(spread, None),
        P(spread, None),
        P(spread, None),
        P(spread),
    )
    out_specs = (P(None, None, spread),) * 3
    return jax.shard_map(
        functools.partial(shards, mesh.shape["tile"], mesh.shape["layer"]),
        mesh=mesh,
        in_specs=in_specs,
        out_specs=out_specs,
        check_vma=False,
    )
```

time: 109 us -> 25.2 us (0.23)
  starting transfers between devices: 32.9 us -> 0 us
  local copies, waits for them, and re-layouts: 36.2 us -> 5.19 us
  other arithmetic: 23.9 us -> 0 us
  Pallas kernels: 0 us -> 19.1 us
  matrix products: 11.6 us -> 0 us
  waiting for transfers between devices: 2.28 us -> 0 us
    pallas_call x0 -> x1, Pallas kernels: none -> 19.1 us  [shards(): pl.pallas_call(functools.partial(kernel, n, nl), out_shape=(jax.ShapeDtyp...]
    ppermute x9 -> x0, starting transfers between devices: 18.8 us -> none  [the longest x4 11.7 us: passed_along(): return lax.ppermute(value, axis, pairs)]
    all_to_all x3 -> x0, starting transfers between devices: 14.2 us -> none  [the longest x2 9.83 us: apply_hop(): lax.all_to_all(paired, 'tile', split_axis=1, concat_axis=1, tiled=True)]
    dot_general x10 -> x0, matrix products: 11.6 us -> none  [the longest x6 8.48 us: hop_forward(): jnp.einsum('rkij,nrkj->nrki', tiles, field_grid, preferred_element_type=j...]
    gather x4 -> x0, local copies, waits for them, and re-layouts: 8.66 us -> none  [the longest x2 4.39 us: apply_hop(): jnp.take(flat_field, recv_sites, axis=1)]
    scatter-add x4 -> x0, other arithmetic: 7.14 us -> none  [the longest x2 3.58 us: apply_hop(): accumulated = accumulated.at[:, send_rows].add(returned_terms)]
    reshape x10 -> x0, local copies, waits for them, and re-layouts: 6.63 us -> none  [the longest x2 2.07 us: apply_hop(): accumulated = accumulated.reshape(field_rows, sites_dev)]
    slice x20 -> x0, local copies, waits for them, and re-layouts: 5.71 us -> none  [the longest x1 2.06 us: shards(): jnp.roll(cheb_one, 2, axis=0)]
  transfers between devices with their start and end apart: 12 -> 0, of which waited for: 2 -> 0; matrix products, arithmetic and copies ran while one was open for 30% -> 0% of each run, Pallas kernels for 0% -> 0%
where the time goes in v1:
time: 25.2 us; the launch traced here: 24.9 us
  Pallas kernels  19.1 us (76%)
  local copies, waits for them, and re-layouts  5.19 us (21%)
  between operations  0.66 us (3%)
    pallas_call x1, Pallas kernels, shards(): pl.pallas_call(functools.partial(kernel, n, nl), out_shape=(jax.ShapeDtyp...  19.1 us
    unnamed x10, local copies, waits for them, and re-layouts  5.19 us

profile of v1, /device:TPU:1, one launch (start us, length us, event | category | flops | bytes accessed | tf_op | source)
XLA Modules:
  0.0 24.9 jit_solution(38435746722360578)
XLA Ops:
  0.6 0.0 copy-start.2
  0.6 0.7 %copy-done.2 = s32[24,2]{0,1:T(2,128)S(1)} copy-done((s32[24,2]{0,1:T(2,128)S(1)}, s32[24,2]{0,1:T(2,128)}, u32[]{:S(2)}) %copy-start.2) | copy-done | bytes 216
  1.3 0.7 %copy.13.pat_ref = s32[24,2]{1,0:T(8,128)} copy(s32[24,2]{0,1:T(2,128)S(1)} %copy-done.2) | data formatting | bytes 384 | tf_op args[4]
  2.0 19.1 %shard_map.121 = (f32[64,3072]{1,0:T(8,128)}, f32[64,3072]{1,0:T(8,128)}, f32[3,4,3072]{2,1,0:T(4,128)}) custom-call(bf16[64,3072]{1,0:T(8,128)(2,1)} %bitcast.6, bf16[24,128,128]{2,1,0:T(8,128)(2,1)} %on_hbm.1, bf16[24,128,128]{2,1,0:T(8,128)(2,1)} %down_hbm.1, bf16[24,128,128]{2,1,0:T(8,128)(2,1)} %right_hbm.1, s32[24,2]{1,0:T(8,128)} %copy.13.pat_ref, ...), custom_call_target="tpu_custom_call" | custom-call | tf_op jit(solution)/shard_map/pallas_call | solution.py:395
  21.1 0.0 copy-start
  21.1 2.1 %copy.17 = f32[4,16,3072]{2,1,0:T(8,128)} copy(f32[4,16,3072]{2,1,0:T(8,128)} %bitcast.5) | data formatting | bytes 1572864
  23.2 0.0 copy-done
  23.2 0.0 copy-start.1
  23.2 0.9 %copy.18 = f32[4,16,3072]{2,1,0:T(8,128)} copy(f32[4,16,3072]{2,1,0:T(8,128)S(1)} %bitcast.4) | data formatting | bytes 1572864
  24.1 0.1 copy-done.1
  24.3 0.7 %copy.19 = f32[3,4,3072]{2,1,0:T(4,128)} copy(f32[3,4,3072]{2,1,0:T(4,128)S(1)} %copy-done.1) | data formatting | bytes 294912
Async XLA Ops:
  0.6 0.7 %copy-start.2 = (s32[24,2]{0,1:T(2,128)S(1)}, s32[24,2]{0,1:T(2,128)}, u32[]{:S(2)}) copy-start(s32[24,2]{0,1:T(2,128)} %param.14) | copy-start | bytes 580
  21.1 2.2 %copy-start = (f32[64,3072]{1,0:T(8,128)S(1)}, f32[64,3072]{1,0:T(8,128)}, u32[]{:S(2)}) copy-start(f32[64,3072]{1,0:T(8,128)} %get-tuple-element.7) | copy-start | bytes 2359300
  23.2 1.0 %copy-start.1 = (f32[3,4,3072]{2,1,0:T(4,128)S(1)}, f32[3,4,3072]{2,1,0:T(4,128)}, u32[]{:S(2)}) copy-start(f32[3,4,3072]{2,1,0:T(4,128)} %get-tuple-element.14) | copy-start | bytes 442372

commit v2 on v1

--- a/solution.py
+++ b/solution.py
@@ -20,6 +20,10 @@
 
 def dot_nt(a, b):
     return lax.dot_general(a, b, (((1,), (1,)), ((), ())), preferred_element_type=F32)
+
+
+def mean(v, comps, vecs):
+    return jnp.sum(v.reshape(comps, vecs, v.shape[1]), axis=1) * (1.0 / vecs)
 
 
 def each(count, body):
@@ -42,22 +46,28 @@
     on_hbm,
     down_hbm,
     right_hbm,
+    pat_hbm,
+    pair_hbm,
+    rows_hbm,
+    target_hbm,
+    weight_hbm,
+    count_hbm,
+    x_ref,
+    one_ref,
+    acc_ref,
+    hot_ref,
+    terms_ref,
+    mom_ref,
     pat_ref,
     pair_ref,
     rows_ref,
     target_ref,
     weight_ref,
     count_ref,
-    one_ref,
-    two_ref,
-    mom_ref,
-    x_ref,
     on_ref,
     down_ref,
     right_ref,
-    acc_ref,
     oneb_ref,
-    hot_ref,
     idx_ref,
     wsend_ref,
     wloc_ref,
@@ -88,15 +98,6 @@
     slots = n * 2 * cap
     wide = TC * tile
 
-    loads = [
-        pltpu.make_async_copy(x_hbm, x_ref, load_sem.at[0]),
-        pltpu.make_async_copy(down_hbm, down_ref, load_sem.at[1]),
-        pltpu.make_async_copy(right_hbm, right_ref, load_sem.at[2]),
-        pltpu.make_async_copy(on_hbm, on_ref, load_sem.at[3]),
-    ]
-    for load in loads:
-        load.start()
-
     has_up = t > 0
     has_low = t < n - 1
     barrier = pltpu.get_barrier_semaphore()
@@ -114,6 +115,22 @@
     def _():
         pl.semaphore_signal(barrier, inc=1, device_id=(t + 1, l), device_id_type=MESH)
 
+    moved = (
+        (rows_hbm, rows_ref),
+        (target_hbm, target_ref),
+        (weight_hbm, weight_ref),
+        (count_hbm, count_ref),
+        (x_hbm, x_ref),
+        (pat_hbm, pat_ref),
+        (down_hbm, down_ref),
+        (right_hbm, right_ref),
+        (on_hbm, on_ref),
+        (pair_hbm, pair_ref),
+    )
+    loads = [pltpu.make_async_copy(a, b, load_sem.at[i]) for i, (a, b) in enumerate(moved)]
+    for load in loads:
+        load.start()
+
     @pl.when(jnp.logical_not(has_up))
     def _():
         up_in[...] = jnp.zeros_like(up_in)
@@ -121,6 +138,9 @@
     @pl.when(jnp.logical_not(has_low))
     def _():
         low_in[...] = jnp.zeros_like(low_in)
+
+    for load in loads[0:4]:
+        load.wait()
 
     sub = lax.broadcasted_iota(jnp.int32, (cap, cap), 0)
     lane = lax.broadcasted_iota(jnp.int32, (cap, cap), 1)
@@ -308,18 +328,19 @@
         both = dot_nn(terms, block(hot_ref, p))
         return both[0:fr] + both[fr : 2 * fr]
 
-    loads[0].wait()
+    loads[4].wait()
     gather(0, x_ref)
-    loads[1].wait()
-    loads[2].wait()
+    for load in loads[5:8]:
+        load.wait()
     for p in range(tiles):
-        down_ref[p] = down_ref[p] * pat_ref[p, 0].astype(F32).astype(BF16)
-        right_ref[p] = right_ref[p] * pat_ref[p, 1].astype(F32).astype(BF16)
+        down_ref[p] = down_ref[p] * pat_ref[0, p].astype(F32).astype(BF16)
+        right_ref[p] = right_ref[p] * pat_ref[1, p].astype(F32).astype(BF16)
     edges(0, x_ref)
     pl.semaphore_wait(barrier, n + 1 + has_up.astype(jnp.int32) + has_low.astype(jnp.int32))
     send_links(0)
     send_edges(0, x_ref)
-    loads[3].wait()
+    loads[8].wait()
+    loads[9].wait()
     local(x_ref)
     receive_edges(0)
     add_edges(0)
@@ -337,24 +358,20 @@
     edges(1, oneb_ref)
     send_edges(1, oneb_ref)
     local(oneb_ref)
+    comps, vecs = mom_ref.shape[1], fr // mom_ref.shape[1]
+    for p in range(tiles):
+        cols = slice(p * tile, (p + 1) * tile)
+        start = x_ref[:, cols].astype(F32)
+        mom_ref[0, :, cols] = mean(start * start, comps, vecs)
+        mom_ref[1, :, cols] = mean(start * one_ref[:, cols], comps, vecs)
     receive_edges(1)
     add_edges(1)
-    terms = link_terms(1)
-    comps, vecs = mom_ref.shape[1], fr // mom_ref.shape[1]
-
-    def mean(v):
-        return jnp.sum(v.reshape(comps, vecs, tile), axis=1) * (1.0 / vecs)
-
     for p in range(tiles):
         cols = slice(p * tile, (p + 1) * tile)
-        hop = acc_ref[:, cols] + scattered(terms, p)
         start = x_ref[:, cols].astype(F32)
-        one = one_ref[:, cols]
-        two = 2.0 * (sign * hop + pair_ref[:, cols] * flipped(one)) - start
-        two_ref[:, cols] = two
-        mom_ref[0, :, cols] = mean(start * start)
-        mom_ref[1, :, cols] = mean(start * one)
-        mom_ref[2, :, cols] = mean(start * two)
+        own = sign * acc_ref[:, cols] + pair_ref[:, cols] * flipped(one_ref[:, cols])
+        acc_ref[:, cols] = 2.0 * own - start
+    terms_ref[...] = link_terms(1)
 
     for rd in range(2):
         each(n, lambda s: link_copy(rd, s, t).wait_send())
@@ -367,6 +384,51 @@
         @pl.when(has_low)
         def _():
             partial_copy(rd).wait_send()
+
+
+def finish(
+    x_ref,
+    one_ref,
+    acc_ref,
+    hot_ref,
+    terms_ref,
+    mom_ref,
+    one_out,
+    two_out,
+    mom_out,
+    two_ref,
+    last_ref,
+    sem,
+):
+    fr, sites = x_ref.shape
+    comps, vecs = mom_ref.shape[1], fr // mom_ref.shape[1]
+    tile = sites // (TR * TC)
+    wide = TC * tile
+    copies = [
+        pltpu.make_async_copy(one_ref, one_out, sem.at[0]),
+        pltpu.make_async_copy(mom_ref, mom_out.at[0:2], sem.at[1]),
+    ]
+    for copy in copies:
+        copy.start()
+    sign = jnp.where(lax.broadcasted_iota(jnp.int32, (fr, tile), 0) < fr // 2, 2.0, -2.0)
+    terms = terms_ref[...]
+    for r in range(TR):
+        for k in range(TC):
+            p = r * TC + k
+            cols = slice(p * tile, (p + 1) * tile)
+            both = dot_nn(terms, hot_ref[:, cols])
+            two = acc_ref[:, cols] + sign * (both[0:fr] + both[fr : 2 * fr])
+            two_ref[:, cols] = two
+            last_ref[:, cols] = mean(x_ref[:, cols].astype(F32) * two, comps, vecs)
+        row = slice(r * wide, (r + 1) * wide)
+        copy = pltpu.make_async_copy(two_ref.at[:, row], two_out.at[:, row], sem.at[2 + r])
+        copy.start()
+        copies.append(copy)
+    copy = pltpu.make_async_copy(last_ref, mom_out.at[2], sem.at[2 + TR])
+    copy.start()
+    copies.append(copy)
+    for copy in copies:
+        copy.wait()
 
 
 def shards(
@@ -390,25 +452,30 @@
     slots = 2 * n * cap
     wide, tall = TC * tile, TR * tile
     vmem = pl.BlockSpec(memory_space=pltpu.VMEM)
-    smem = pl.BlockSpec(memory_space=pltpu.SMEM)
-    hbm = pl.BlockSpec(memory_space=pl.ANY)
-    one, two, moments = pl.pallas_call(
+    hbm = pl.BlockSpec(memory_space=pltpu.HBM)
+    stage = pl.pallas_call(
         functools.partial(kernel, n, nl),
         out_shape=(
-            jax.ShapeDtypeStruct((fr, sites), F32),
-            jax.ShapeDtypeStruct((fr, sites), F32),
-            jax.ShapeDtypeStruct((3, comps, sites), F32),
+            pltpu.VMEM((fr, sites), BF16),
+            pltpu.VMEM((fr, sites), F32),
+            pltpu.VMEM((fr, sites), F32),
+            pltpu.VMEM((slots, sites), BF16),
+            pltpu.VMEM((2 * fr, slots), BF16),
+            pltpu.VMEM((2, comps, sites), F32),
         ),
-        in_specs=[hbm, hbm, hbm, hbm, smem, vmem, vmem, vmem, vmem, smem],
-        out_specs=(vmem, vmem, vmem),
+        in_specs=[hbm] * 10,
+        out_specs=(vmem,) * 6,
         scratch_shapes=[
-            pltpu.VMEM((fr, sites), BF16),
+            pltpu.SMEM((2, tiles), jnp.int32),
+            pltpu.VMEM((1, sites), F32),
+            pltpu.VMEM((n, cap), jnp.int32),
+            pltpu.VMEM((n, cap), jnp.int32),
+            pltpu.VMEM((n, cap), BF16),
+            pltpu.SMEM((n,), jnp.int32),
             pltpu.VMEM((tiles, tile, tile), BF16),
             pltpu.VMEM((tiles, tile, tile), BF16),
             pltpu.VMEM((tiles, tile, tile), BF16),
-            pltpu.VMEM((fr, sites), F32),
             pltpu.VMEM((fr, sites), BF16),
-            pltpu.VMEM((slots, sites), BF16),
             pltpu.VMEM((slots, tile), jnp.int32),
             pltpu.VMEM((slots, 2 * fr), F32),
             pltpu.VMEM((slots, 2 * fr), F32),
@@ -421,27 +488,48 @@
             pltpu.VMEM((2, fr, wide), BF16),
             pltpu.VMEM((2, fr, tall), BF16),
             pltpu.VMEM((2, fr, tall), BF16),
-            pltpu.SemaphoreType.DMA((4,)),
+            pltpu.SemaphoreType.DMA((10,)),
             pltpu.SemaphoreType.DMA((2, n)),
             pltpu.SemaphoreType.DMA((2, n)),
             pltpu.SemaphoreType.DMA((2, 3)),
             pltpu.SemaphoreType.DMA((2, 3)),
         ],
         compiler_params=pltpu.CompilerParams(
-            collective_id=0, has_side_effects=True, vmem_limit_bytes=56 * 1024 * 1024
+            collective_id=0, has_side_effects=True, vmem_limit_bytes=30 * 1024 * 1024
         ),
     )(
-        rand_vectors.reshape(fr, sites),
-        onsite,
-        down_hop,
-        right_hop,
-        pattern,
-        pairing.reshape(1, sites),
-        link_rows,
-        link_target,
-        link_weight,
-        link_count,
+        *[
+            pltpu.with_memory_space_constraint(operand, pltpu.HBM)
+            for operand in (
+                rand_vectors.reshape(fr, sites),
+                onsite,
+                down_hop,
+                right_hop,
+                pattern.T,
+                pairing.reshape(1, sites),
+                link_rows,
+                link_target,
+                link_weight,
+                link_count,
+            )
+        ]
     )
+    one, two, moments = pl.pallas_call(
+        finish,
+        out_shape=(
+            jax.ShapeDtypeStruct((fr, sites), F32),
+            jax.ShapeDtypeStruct((fr, sites), F32),
+            jax.ShapeDtypeStruct((3, comps, sites), F32),
+        ),
+        in_specs=[vmem] * 6,
+        out_specs=(hbm,) * 3,
+        scratch_shapes=[
+            pltpu.VMEM((fr, sites), F32),
+            pltpu.VMEM((comps, sites), F32),
+            pltpu.SemaphoreType.DMA((3 + TR,)),
+        ],
+        compiler_params=pltpu.CompilerParams(vmem_limit_bytes=8 * 1024 * 1024),
+    )(*stage)
     return (
         one.reshape(comps, vecs, sites),
         two.reshape(comps, vecs, sites),

time: 25.2 us -> 18.5 us (0.73)
  local copies, waits for them, and re-layouts: 5.19 us -> 0 us
  Pallas kernels: 19.1 us -> 17.6 us
    unnamed x10 -> x0, local copies, waits for them, and re-layouts: 5.19 us -> none
    pallas_call x1 -> x2, Pallas kernels: 19.1 us -> 17.6 us  [the longest x1 16.4 us: shards(): pl.pallas_call(functools.partial(kernel, n, nl), out_shape=(pltpu.VMEM((f...]
where the time goes in v2:
time: 18.5 us; the launch traced here: 18.3 us
  Pallas kernels  17.6 us (95%)
  between operations  0.64 us (3%)
    pallas_call x1, Pallas kernels, shards(): pl.pallas_call(functools.partial(kernel, n, nl), out_shape=(pltpu.VMEM((f...  16.4 us
    pallas_call x1, Pallas kernels, shards(): pl.pallas_call(finish, out_shape=(jax.ShapeDtypeStruct((fr, sites), F32),...  1.24 us

profile of v2, /device:TPU:1, one launch (start us, length us, event | category | flops | bytes accessed | tf_op | source)
XLA Modules:
  0.0 18.3 jit_solution(8260271091673920207)
XLA Ops:
  0.6 16.4 %shard_map.121 = (bf16[64,3072]{1,0:T(8,128)(2,1)S(1)}, f32[64,3072]{1,0:T(8,128)S(1)}, f32[64,3072]{1,0:T(8,128)S(1)}, bf16[128,3072]{1,0:T(8,128)(2,1)S(1)}, b...) custom-call(bf16[64,3072]{1,0:T(8,128)(2,1)} %bitcast.5, bf16[24,128,128]{2,1,0:T(8,128)(2,1)} %on_hbm.1, ...), custom_call_target="tpu_custom_call" | custom-call | tf_op jit(solution)/shard_map/pallas_call | solution.py:456
  17.0 1.2 %shard_map.122 = (f32[64,3072]{1,0:T(8,128)}, f32[64,3072]{1,0:T(8,128)}, f32[3,4,3072]{2,1,0:T(4,128)}) custom-call(bf16[64,3072]{1,0:T(8,128)(2,1)S(1)} %get-tuple-element.12.x_ref, f32[64,3072]{1,0:T(8,128)S(1)} %get-tuple-element.13.one_ref, f32[64,3072]{1,0:T(8,128)S(1)} %get-tuple-element.14.acc_ref, bf16[128,3072]{1,0:T(8,128)(2,1)S(1)} %get-tuple-element.15.hot_ref, ...), custom_call_target="tpu_custom_call" | custom-call | tf_op jit(solution)/shard_map/pallas_call | solution.py:517

commit v3 on v2

--- a/solution.py
+++ b/solution.py
@@ -72,6 +72,8 @@
     wsend_ref,
     wloc_ref,
     gath_ref,
+    meet_ref,
+    parts_ref,
     wide_ref,
     sbuf,
     lbuf,
@@ -221,9 +223,10 @@
             device_id_type=MESH,
         )
 
-    def gather(rd, src):
+    def gather(src):
         gath_ref[:, 0:fr] = dot_nt(hot_ref[...], src[...])
 
+    def fill_links(rd):
         def fill(s):
             base = s * (2 * cap)
             both = jnp.concatenate(
@@ -232,6 +235,20 @@
             sbuf[rd, s] = (both + wsend_ref[pl.ds(base, 2 * cap), :]).astype(BF16)
 
         each(n, fill)
+
+    def meets():
+        step = tile if slots % tile == 0 else slots
+        count = slots // step
+
+        def meet(i, j):
+            rows = pl.ds(pl.multiple_of(i * step, step), step)
+            cols = pl.ds(pl.multiple_of(j * step, step), step)
+            meet_ref[rows, cols] = dot_nt(hot_ref[rows, :], hot_ref[cols, :]).astype(BF16)
+
+        if count == 1:
+            meet_ref[...] = dot_nt(hot_ref[...], hot_ref[...]).astype(BF16)
+        else:
+            each(count, lambda i: lax.fori_loop(0, count, lambda j, c: (meet(i, j), c)[1], 0))
 
     def edges(rd, src):
         for k in range(TC):
@@ -329,7 +346,8 @@
         return both[0:fr] + both[fr : 2 * fr]
 
     loads[4].wait()
-    gather(0, x_ref)
+    gather(x_ref)
+    fill_links(0)
     for load in loads[5:8]:
         load.wait()
     for p in range(tiles):
@@ -342,19 +360,34 @@
     loads[8].wait()
     loads[9].wait()
     local(x_ref)
+    meets()
     receive_edges(0)
     add_edges(0)
-    terms = link_terms(0)
     for p in range(tiles):
         cols = slice(p * tile, (p + 1) * tile)
-        hop = acc_ref[:, cols] + scattered(terms, p)
         start = x_ref[:, cols].astype(F32)
-        one = sign * hop + pair_ref[:, cols] * flipped(start)
+        value = sign * acc_ref[:, cols] + pair_ref[:, cols] * flipped(start)
+        acc_ref[:, cols] = value
+        for i in range(3):
+            part = value.astype(BF16)
+            parts_ref[i * fr : (i + 1) * fr, cols] = part
+            value = value - part.astype(F32)
+    three = dot_nt(parts_ref[...], hot_ref[...])
+    at_slots = three[0:fr] + three[fr : 2 * fr] + three[2 * fr :]
+    terms = link_terms(0)
+    both = dot_nn(terms, meet_ref[...])
+    met = both[0:fr] + both[fr : 2 * fr]
+    signs = jnp.where(lax.broadcasted_iota(jnp.int32, (fr, slots), 0) < fr // 2, 1.0, -1.0)
+    ends = at_slots + signs * met
+    gath_ref[...] = jnp.concatenate([ends, jnp.zeros_like(ends)], axis=0).T
+    fill_links(1)
+    send_links(1)
+    for p in range(tiles):
+        cols = slice(p * tile, (p + 1) * tile)
+        one = acc_ref[:, cols] + sign * scattered(terms, p)
         one_ref[:, cols] = one
         oneb_ref[:, cols] = one.astype(BF16)
 
-    gather(1, oneb_ref)
-    send_links(1)
     edges(1, oneb_ref)
     send_edges(1, oneb_ref)
     local(oneb_ref)
@@ -480,6 +513,8 @@
             pltpu.VMEM((slots, 2 * fr), F32),
             pltpu.VMEM((slots, 2 * fr), F32),
             pltpu.VMEM((slots, 2 * fr), F32),
+            pltpu.VMEM((slots, slots), BF16),
+            pltpu.VMEM((3 * fr, sites), BF16),
             pltpu.VMEM((n, cap), F32),
             pltpu.VMEM((2, n, 2 * cap, 2 * fr), BF16),
             pltpu.VMEM((2, n, 2 * cap, 2 * fr), BF16),
@@ -495,7 +530,7 @@
             pltpu.SemaphoreType.DMA((2, 3)),
         ],
         compiler_params=pltpu.CompilerParams(
-            collective_id=0, has_side_effects=True, vmem_limit_bytes=30 * 1024 * 1024
+            collective_id=0, has_side_effects=True, vmem_limit_bytes=44 * 1024 * 1024
         ),
     )(
         *[

time: 18.5 us -> 19.1 us (1.032)
  Pallas kernels: 17.6 us -> 18.1 us
    pallas_call x1, Pallas kernels: 16.4 us -> 16.9 us  [shards(): pl.pallas_call(functools.partial(kernel, n, nl), out_shape=(pltpu.VMEM((f...]
where the time goes in v3:
time: 19.1 us; the launch traced here: 18.7 us
  Pallas kernels  18.1 us (95%)
  between operations  0.64 us (3%)
    pallas_call x1, Pallas kernels, shards(): pl.pallas_call(functools.partial(kernel, n, nl), out_shape=(pltpu.VMEM((f...  16.9 us
    pallas_call x1, Pallas kernels, shards(): pl.pallas_call(finish, out_shape=(jax.ShapeDtypeStruct((fr, sites), F32),...  1.24 us

profile of v3, /device:TPU:1, one launch (start us, length us, event | category | flops | bytes accessed | tf_op | source)
XLA Modules:
  0.0 18.7 jit_solution(3374947760237264543)
XLA Ops:
  0.6 16.9 %shard_map.121 = (bf16[64,3072]{1,0:T(8,128)(2,1)S(1)}, f32[64,3072]{1,0:T(8,128)S(1)}, f32[64,3072]{1,0:T(8,128)S(1)}, bf16[128,3072]{1,0:T(8,128)(2,1)S(1)}, b...) custom-call(bf16[64,3072]{1,0:T(8,128)(2,1)} %bitcast.5, bf16[24,128,128]{2,1,0:T(8,128)(2,1)} %on_hbm.1, ...), custom_call_target="tpu_custom_call" | custom-call | tf_op jit(solution)/shard_map/pallas_call | solution.py:489
  17.5 1.2 %shard_map.122 = (f32[64,3072]{1,0:T(8,128)}, f32[64,3072]{1,0:T(8,128)}, f32[3,4,3072]{2,1,0:T(4,128)}) custom-call(bf16[64,3072]{1,0:T(8,128)(2,1)S(1)} %get-tuple-element.12.x_ref, f32[64,3072]{1,0:T(8,128)S(1)} %get-tuple-element.13.one_ref, f32[64,3072]{1,0:T(8,128)S(1)} %get-tuple-element.14.acc_ref, bf16[128,3072]{1,0:T(8,128)(2,1)S(1)} %get-tuple-element.15.hot_ref, ...), custom_call_target="tpu_custom_call" | custom-call | tf_op jit(solution)/shard_map/pallas_call | solution.py:552
